TPU v7x, 256 devices: a whole 4x4x8 slice. The times are simulated.
256 devices in a mesh: docs: 32 (over x, z), topics: 8 (over y, core).
Axes of the slice: x: 4, y: 4, z: 8, core: 2. Of those that a mesh axis runs over, the one named last changes fastest.
Arguments:
- log_beta: bfloat16 [262144, 2048], P('docs', 'topics'), may hold values from -250 to -4
- gamma_init: float32 [512, 2048], P('docs', 'topics'), may hold values from 0.05 to 5
- topic_prior: float32 [2048], P('topics'), may hold values from 0.02 to 0.5
- word_block: int32 [512, 256, 1], P('docs'), may hold values from 0 to 31; in each aligned block of 4096 rows (0 to 4095, 4096 to 8191, ..., all dimensions but the last counted through in order) at most 256 rows name the same one
- word_row: int32 [512, 256], P('docs'), may hold values from 0 to 8191
- counts: int32 [512, 256], P('docs'), may hold values from 0 to 2
Outputs:
- doc_gamma: float32 [512, 2048], P('docs', 'topics')
- sstats: float32 [262144, 2048], P('docs', 'topics')
Inputs may be any that keep to these rules, and one draw needn't show every extreme that they name: `word_block`: among the token slots of one device's 16 documents, at most 256 name the same vocabulary block, and some block is named by exactly 256 of them on some device. `counts`: A count of 0 marks an empty slot.
All inputs are finite; a program needn't handle non-finite values.
Results may differ from a plain program's by a relative error of at most 0.0003.
Values may be sent and summed in bfloat16 or wider, within the bound.
A program may use at most 64 MiB of HBM per device.

v0:
```python
import jax
import jax.numpy as jnp
from jax import lax
from jax.sharding import PartitionSpec as P

ITERS = 3


def copy_for_each(array, axis):
    devices = lax.axis_size(axis)
    return lax.all_to_all(
        jnp.broadcast_to(array[None], (devices, *array.shape)), axis, 0, 0, tiled=True
    )


def all_in_one(array, axis):
    leaves = jax.tree.leaves(array)
    sequence = sorted(range(len(leaves)), key=lambda k: -leaves[k].size)
    width = (1, *leaves[sequence[0]].shape)[-1]
    lines = [
        jnp.pad(leaves[k].reshape(-1), (0, -leaves[k].size % width)).reshape(-1, width)
        for k in sequence
    ]
    both, at, found = (copy_for_each(jnp.concatenate(lines), axis), 0, {})
    for k, line in zip(sequence, lines):
        share = both[:, at : at + len(line)].reshape(len(both), -1)
        found[k] = share[:, : leaves[k].size].reshape(-1, *leaves[k].shape)
        at += len(line)
    numbers = iter(range(len(leaves)))
    return jax.tree.map(lambda _: found[next(numbers)], array)


def collected_alike(array, axis):
    leaves, found = (jax.tree.leaves(array), {})
    for initial, a in enumerate(leaves):
        if initial not in found:
            alike = [k for k, b in enumerate(leaves) if b.dtype == a.dtype]
            got = (
                all_in_one([leaves[k] for k in alike], axis)
                if len(alike) > 1
                else [copy_for_each(a, axis)]
            )
            for k, b in zip(alike, got):
                found[k] = b
    numbers = iter(range(len(leaves)))
    return jax.tree.map(lambda _: found[next(numbers)], array)


def joined_by_halves(pieces, combine):
    while len(jax.tree.leaves(pieces)[0]) > 1:
        pieces = jax.vmap(combine)(
            *(jax.tree.map(lambda part: part[side::2], pieces) for side in (0, 1))
        )
    return jax.tree.map(lambda part: part[0], pieces)


def joined_all(array, axis, combine):
    pieces = collected_alike(array, axis)
    return joined_by_halves(pieces, combine)


def in_order(blocks, dim):
    shape = list(blocks.shape[1:])
    shape[dim] *= blocks.shape[0]
    return jnp.moveaxis(blocks, 0, dim).reshape(shape)


def gathered_copies(array, axis, dim):
    blocks = copy_for_each(array, axis)
    return in_order(blocks, dim)


def join_pairs(first, second):
    row_max = jnp.maximum(first[0], second[0])
    return (
        row_max,
        first[1] * jnp.exp(first[0] - row_max) + second[1] * jnp.exp(second[0] - row_max),
    )


def slot_places(word_owner, owners, capacity):
    length = word_owner.shape[1]
    member = (word_owner[:, None, :] == jnp.arange(owners, dtype=jnp.int32)[None, :, None]).astype(
        jnp.float32
    )
    earlier = (jnp.arange(length)[:, None] > jnp.arange(length)[None, :]).astype(jnp.float32)
    before = jnp.einsum("dom,nm->don", member, earlier, precision=lax.Precision.HIGHEST)
    per_doc = jnp.sum(member, axis=2)
    offset = jnp.cumsum(per_doc, axis=0) - per_doc
    slot_rank = jnp.sum(member * (before + offset[:, :, None]), axis=1)
    return word_owner * capacity + slot_rank.astype(jnp.int32)


def normalized(log_theta, token_rows):
    scores = log_theta[:, None, :] + token_rows.astype(jnp.float32)
    row_max = jnp.max(scores, axis=2)
    exp_mass = jnp.sum(jnp.exp(scores - row_max[:, :, None]), axis=2)
    row_max, exp_mass = joined_all((row_max, exp_mass), "topics", join_pairs)
    return (scores, row_max + jnp.log(exp_mass))


def per_device(log_beta, gamma_init, topic_prior, word_block, word_row, counts):
    doc_rows, length = counts.shape
    topic_cols = log_beta.shape[1]
    owners = lax.axis_size("docs")
    tokens = doc_rows * length
    capacity = 2 * tokens // owners
    weight = counts.astype(jnp.float32)
    places = slot_places(word_block[:, :, 0], owners, capacity).reshape(tokens)
    holder = jnp.arange(doc_rows, dtype=jnp.int32)[:, None] + jnp.zeros((1, length), jnp.int32)
    blank_ids = jnp.zeros((owners * capacity,), jnp.int32)
    requests = (
        blank_ids.at[places].set(word_row.reshape(tokens)).reshape(owners, capacity),
        blank_ids.at[places].set(holder.reshape(tokens)).reshape(owners, capacity),
        blank_ids.at[places].set(counts.reshape(tokens)).reshape(owners, capacity),
    )
    request = (
        lax.all_to_all(requests[0], "docs", split_axis=0, concat_axis=0, tiled=True),
        lax.all_to_all(requests[1], "docs", split_axis=0, concat_axis=0, tiled=True),
        lax.all_to_all(requests[2], "docs", split_axis=0, concat_axis=0, tiled=True),
    )
    found_rows = log_beta[request[0]]
    returned = lax.all_to_all(found_rows, "docs", split_axis=0, concat_axis=0, tiled=True)
    fetched, found_rows, own_rows, own_docs, own_counts = (
        returned,
        found_rows,
        request[0],
        request[1],
        request[2],
    )
    token_rows = fetched.reshape(owners * capacity, topic_cols)[places].reshape(
        doc_rows, length, topic_cols
    )
    doc_gamma = gamma_init
    for sweep_index in range(ITERS + 1):
        log_theta = lax.digamma(doc_gamma)
        scores, log_norm = normalized(log_theta, token_rows)
        topic_share = jnp.exp(scores - log_norm[:, :, None])
        if sweep_index < ITERS:
            doc_gamma = topic_prior[None, :] + jnp.einsum(
                "dn,dnk->dk", weight, topic_share, precision=lax.Precision.HIGHEST
            )
    theta_all = gathered_copies(log_theta, "docs", 0)
    norm_slots = (
        jnp.zeros((owners * capacity,), jnp.float32)
        .at[places]
        .set(log_norm.reshape(tokens))
        .reshape(owners, capacity)
    )
    norm_back = lax.all_to_all(norm_slots, "docs", split_axis=0, concat_axis=0, tiled=True)
    source = jnp.arange(owners, dtype=jnp.int32)[:, None] * doc_rows + own_docs
    rescored = theta_all[source] + found_rows.astype(jnp.float32)
    stat_terms = own_counts.astype(jnp.float32)[:, :, None] * jnp.exp(
        rescored - norm_back[:, :, None]
    )
    sstats = (
        jnp.zeros((log_beta.shape[0], topic_cols), jnp.float32)
        .at[own_rows.reshape(-1)]
        .add(stat_terms.reshape(-1, topic_cols))
    )
    return (doc_gamma, sstats)


def solution(mesh):
    in_specs = (
        P("docs", "topics"),
        P("docs", "topics"),
        P("topics"),
        P("docs", None, None),
        P("docs", None),
        P("docs", None),
    )
    out_specs = (P("docs", "topics"), P("docs", "topics"))
    return jax.shard_map(
        per_device, mesh=mesh, in_specs=in_specs, out_specs=out_specs, check_vma=False
    )
```

profile of v0, /device:TPU:2, one launch (start us, length us, event | category | flops | bytes accessed | tf_op | source)
XLA Modules:
  0.0 443.0 jit_solution(2294478252793602568)
XLA Ops:
  3.4 15.5 %scatter_custom_fusion = s32[8192]{0:T(1024)S(1)} fusion(s32[4096]{0:T(1024)S(1)} %bitcast.91, s32[4096]{0:T(1024)S(1)} %bitcast.103, s32[]{:T(128)} %constant.28.clone.1), kind=kCustom, calls=%fused_computation.145 | custom fusion | bytes 32772 | tf_op jit(solution)/shard_map/scatter | solution.py:113
  19.0 20.1 %all_to_all.72 = s32[32,1,256]{2,1,0:T(1,128)S(1)} all-to-all(s32[32,1,256]{2,1,0:T(1,128)S(1)} %bitcast.89), channel_id=1, replica_groups=mesh['docs'=32,'topics'=8] {'docs'}, dimensions={0} | all-to-all | bytes 65536 | tf_op jit(solution)/shard_map/all_to_all | solution.py:118
  39.1 33.6 %gather_fusion = bf16[8192,256]{1,0:T(8,128)(2,1)} fusion(bf16[8192,256]{1,0:T(8,128)(2,1)} %param.6, s32[8192]{0:T(1024)S(1)} %broadcast_clamp_fusion.1), kind=kCustom, calls=%fused_computation | custom fusion | bytes 8421376 | tf_op jit(solution)/shard_map/gather | solution.py:122
  72.7 6.1 %all-to-all-start.1 = ((bf16[32,256,256]{2,1,0:T(8,128)(2,1)}), bf16[32,256,256]{2,1,0:T(8,128)(2,1)}, u32[]{:S(2)}, u32[]{:S(2)}) async-start(bf16[32,256,256]{2,1,0:T(8,128)(2,1)} %bitcast.82), calls=%async_computation.1 | async-start | bytes 8388608 | tf_op jit(solution)/shard_map/all_to_all | solution.py:123
  79.0 92.7 %all-to-all-done.1 = bf16[32,256,256]{2,1,0:T(8,128)(2,1)} async-done(((bf16[32,256,256]{2,1,0:T(8,128)(2,1)}), bf16[32,256,256]{2,1,0:T(8,128)(2,1)}, u32[]{:S(2)}, u32[]{:S(2)}) %all-to-all-start.1) | async-done | bytes 4194336 | tf_op jit(solution)/shard_map/all_to_all | solution.py:123
  171.6 15.7 %gather_fusion.1 = bf16[4096,256]{1,0:T(8,128)(2,1)S(1)} fusion(bf16[8192,256]{1,0:T(8,128)(2,1)} %bitcast.7, s32[4096]{0:T(1024)S(1)} %broadcast_clamp_fusion.2), kind=kCustom, calls=%fused_computation.1 | custom fusion | bytes 4210688 | tf_op jit(solution)/shard_map/gather | solution.py:131
  190.3 4.5 %all-to-all-start.2 = ((f32[8,32,256]{2,1,0:T(8,128)}), f32[8,32,256]{2,1,0:T(8,128)S(1)}, u32[]{:S(2)}, u32[]{:S(2)}) async-start(f32[8,32,256]{2,1,0:T(8,128)} %broadcast_in_dim.14), calls=%async_computation.2 | async-start | bytes 524288 | tf_op jit(solution)/shard_map/all_to_all | solution.py:11
  194.8 7.5 %all-to-all-done.2 = f32[8,32,256]{2,1,0:T(8,128)S(1)} async-done(((f32[8,32,256]{2,1,0:T(8,128)}), f32[8,32,256]{2,1,0:T(8,128)S(1)}, u32[]{:S(2)}, u32[]{:S(2)}) %all-to-all-start.2) | async-done | bytes 262176 | tf_op jit(solution)/shard_map/all_to_all | solution.py:11
  207.8 9.9 %all_to_all.73 = f32[8,32,256]{2,1,0:T(8,128)S(1)} all-to-all(f32[8,32,256]{2,1,0:T(8,128)S(1)} %broadcast_in_dim.15), channel_id=1, replica_groups=mesh['docs'=32,'topics'=8] {'topics'}, dimensions={0} | all-to-all | bytes 524288 | tf_op jit(solution)/shard_map/all_to_all | solution.py:11
  224.0 3.4 all-to-all-start.4
  227.5 16.1 %scatter_custom_fusion.2 = s32[8192]{0:T(1024)} fusion(s32[4096]{0:T(1024)S(1)} %bitcast.93, s32[4096]{0:T(1024)S(1)} %bitcast.105, s32[]{:T(128)} %constant.28.clone.1), kind=kCustom, calls=%fused_computation.141 | custom fusion | bytes 32772 | tf_op jit(solution)/shard_map/scatter | solution.py:114
  243.6 16.1 %scatter_custom_fusion.1 = s32[8192]{0:T(1024)} fusion(s32[4096]{0:T(1024)S(1)} %bitcast.94, s32[4096]{0:T(1024)S(1)} %bitcast.106, s32[]{:T(128)} %constant.28.clone.1), kind=kCustom, calls=%fused_computation.143 | custom fusion | bytes 32772 | tf_op jit(solution)/shard_map/scatter | solution.py:115
  259.7 7.9 %all-to-all-start.7 = ((s32[32,1,256]{2,1,0:T(1,128)}), s32[32,1,256]{2,1,0:T(1,128)S(1)}, u32[]{:S(2)}, u32[]{:S(2)}) async-start(s32[32,1,256]{2,1,0:T(1,128)} %bitcast.21), calls=%async_computation.7 | async-start | bytes 65536 | tf_op jit(solution)/shard_map/all_to_all | solution.py:119
  276.3 7.1 %all-to-all-start.5 = ((s32[32,1,256]{2,1,0:T(1,128)}), s32[32,1,256]{2,1,0:T(1,128)S(1)}, u32[]{:S(2)}, u32[]{:S(2)}) async-start(s32[32,1,256]{2,1,0:T(1,128)} %bitcast.18), calls=%async_computation.5 | async-start | bytes 65536 | tf_op jit(solution)/shard_map/all_to_all | solution.py:120
  283.4 8.7 %all-to-all-done.5 = s32[32,1,256]{2,1,0:T(1,128)S(1)} async-done(((s32[32,1,256]{2,1,0:T(1,128)}), s32[32,1,256]{2,1,0:T(1,128)S(1)}, u32[]{:S(2)}, u32[]{:S(2)}) %all-to-all-start.5) | async-done | bytes 32800 | tf_op jit(solution)/shard_map/all_to_all | solution.py:120
  292.8 4.7 %all-to-all-start.8 = ((f32[8,32,256]{2,1,0:T(8,128)}), f32[8,32,256]{2,1,0:T(8,128)S(1)}, u32[]{:S(2)}, u32[]{:S(2)}) async-start(f32[8,32,256]{2,1,0:T(8,128)} %broadcast_in_dim.20), calls=%async_computation.8 | async-start | bytes 524288 | tf_op jit(solution)/shard_map/all_to_all | solution.py:11
  297.7 7.4 %all-to-all-done.8 = f32[8,32,256]{2,1,0:T(8,128)S(1)} async-done(((f32[8,32,256]{2,1,0:T(8,128)}), f32[8,32,256]{2,1,0:T(8,128)S(1)}, u32[]{:S(2)}, u32[]{:S(2)}) %all-to-all-start.8) | async-done | bytes 262176 | tf_op jit(solution)/shard_map/all_to_all | solution.py:11
  305.9 5.1 %all-to-all-start.6 = ((f32[32,16,256]{2,1,0:T(8,128)}), f32[32,16,256]{2,1,0:T(8,128)S(1)}, u32[]{:S(2)}, u32[]{:S(2)}) async-start(f32[32,16,256]{2,1,0:T(8,128)} %broadcast_in_dim.18), calls=%async_computation.6 | async-start | bytes 1048576 | tf_op jit(solution)/shard_map/all_to_all | solution.py:11
  311.2 16.1 %scatter_custom_fusion.3 = f32[8192]{0:T(1024)} fusion(s32[4096]{0:T(1024)S(1)} %bitcast.95, f32[4096]{0:T(1024)S(1)} %bitcast.104, f32[]{:T(128)} %constant.30.clone.1), kind=kCustom, calls=%fused_computation.130 | custom fusion | bytes 32772 | tf_op jit(solution)/shard_map/scatter | solution.py:147
  327.2 9.9 %all-to-all-start.9 = ((f32[32,1,256]{2,1,0:T(1,128)}), f32[32,1,256]{2,1,0:T(1,128)S(1)}, u32[]{:S(2)}, u32[]{:S(2)}) async-start(f32[32,1,256]{2,1,0:T(1,128)} %bitcast.27), calls=%async_computation.9 | async-start | bytes 65536 | tf_op jit(solution)/shard_map/all_to_all | solution.py:150
  337.1 31.5 %gather_fusion.2 = f32[8192,256]{1,0:T(8,128)} fusion(f32[512,256]{1,0:T(8,128)S(1)} %bitcast.70, s32[8192]{0:T(1024)S(1)} %broadcast_clamp_fusion), kind=kCustom, calls=%fused_computation.2 | custom fusion | bytes 16809984 | tf_op jit(solution)/shard_map/gather | solution.py:152
  368.6 9.5 %convert_add_fusion = f32[32,256,256]{2,1,0:T(8,128)} fusion(f32[32,256,256]{2,1,0:T(8,128)} %bitcast.84, bf16[32,256,256]{2,1,0:T(8,128)(2,1)} %bitcast.83), kind=kLoop, calls=%fused_computation.11 | loop fusion | flops 4194304 | bytes 20971520 | tf_op jit(solution)/shard_map/add | solution.py:152
  378.1 7.9 %fusion.1 = f32[8192,256]{1,0:T(8,128)} fusion(f32[32,256,256]{2,1,0:T(8,128)} %convert_add_fusion, f32[8192]{0:T(1024)S(1)} %bitcast.87, f32[8192]{0:T(1024)S(1)} %bitcast.86), kind=kLoop, calls=%fused_computation.10 | loop fusion | flops 4194304 | bytes 16842752 | tf_op jit(solution)/shard_map/mul | solution.py:153
  386.0 56.9 %scatter_custom_fusion.4 = f32[8192,256]{1,0:T(8,128)} fusion(s32[8192]{0:T(1024)S(1)} %bitcast.101, f32[8192,256]{1,0:T(8,128)} %fusion.1, f32[]{:T(128)} %constant.30.clone.1), kind=kCustom, calls=%fused_computation.41 | custom fusion | flops 2097152 | bytes 8389120 | tf_op jit(solution)/shard_map/scatter-add | solution.py:159
  (73 shorter events, 28.1 us)
Async XLA Ops:
  72.7 6.1 %copy-start.1 = (f32[16,256]{1,0:T(8,128)S(1)}, f32[16,256]{1,0:T(8,128)}, u32[]{:S(2)}) copy-start(f32[16,256]{1,0:T(8,128)} %param.7) | copy-start | bytes 49156
  72.7 98.9 %all-to-all-start.1 = ((bf16[32,256,256]{2,1,0:T(8,128)(2,1)}), bf16[32,256,256]{2,1,0:T(8,128)(2,1)}, u32[]{:S(2)}, u32[]{:S(2)}) async-start(bf16[32,256,256]{2,1,0:T(8,128)(2,1)} %bitcast.82), calls=%async_computation.1 | async-start | bytes 8388608 | tf_op jit(solution)/shard_map/all_to_all | solution.py:123
  187.4 7.4 %copy-start = (s32[16,256]{1,0:T(8,128)S(1)}, s32[16,256]{1,0:T(8,128)}, u32[]{:S(2)}) copy-start(s32[16,256]{1,0:T(8,128)} %param.11) | copy-start | bytes 49156
  188.1 17.5 %copy-start.2 = (f32[256]{0:T(256)S(1)}, f32[256]{0:T(256)}, u32[]{:S(2)}) copy-start(f32[256]{0:T(256)} %param.8) | copy-start | bytes 3076
  190.3 12.0 %all-to-all-start.2 = ((f32[8,32,256]{2,1,0:T(8,128)}), f32[8,32,256]{2,1,0:T(8,128)S(1)}, u32[]{:S(2)}, u32[]{:S(2)}) async-start(f32[8,32,256]{2,1,0:T(8,128)} %broadcast_in_dim.14), calls=%async_computation.2 | async-start | bytes 524288 | tf_op jit(solution)/shard_map/all_to_all | solution.py:11
  224.0 35.7 %all-to-all-start.4 = ((f32[8,32,256]{2,1,0:T(8,128)}), f32[8,32,256]{2,1,0:T(8,128)S(1)}, u32[]{:S(2)}, u32[]{:S(2)}) async-start(f32[8,32,256]{2,1,0:T(8,128)} %broadcast_in_dim.16), calls=%async_computation.4 | async-start | bytes 524288 | tf_op jit(solution)/shard_map/all_to_all | solution.py:11
  259.7 16.6 %all-to-all-start.7 = ((s32[32,1,256]{2,1,0:T(1,128)}), s32[32,1,256]{2,1,0:T(1,128)S(1)}, u32[]{:S(2)}, u32[]{:S(2)}) async-start(s32[32,1,256]{2,1,0:T(1,128)} %bitcast.21), calls=%async_computation.7 | async-start | bytes 65536 | tf_op jit(solution)/shard_map/all_to_all | solution.py:119
  276.3 15.8 %all-to-all-start.5 = ((s32[32,1,256]{2,1,0:T(1,128)}), s32[32,1,256]{2,1,0:T(1,128)S(1)}, u32[]{:S(2)}, u32[]{:S(2)}) async-start(s32[32,1,256]{2,1,0:T(1,128)} %bitcast.18), calls=%async_computation.5 | async-start | bytes 65536 | tf_op jit(solution)/shard_map/all_to_all | solution.py:120
  292.8 12.2 %all-to-all-start.8 = ((f32[8,32,256]{2,1,0:T(8,128)}), f32[8,32,256]{2,1,0:T(8,128)S(1)}, u32[]{:S(2)}, u32[]{:S(2)}) async-start(f32[8,32,256]{2,1,0:T(8,128)} %broadcast_in_dim.20), calls=%async_computation.8 | async-start | bytes 524288 | tf_op jit(solution)/shard_map/all_to_all | solution.py:11
  305.9 21.4 %all-to-all-start.6 = ((f32[32,16,256]{2,1,0:T(8,128)}), f32[32,16,256]{2,1,0:T(8,128)S(1)}, u32[]{:S(2)}, u32[]{:S(2)}) async-start(f32[32,16,256]{2,1,0:T(8,128)} %broadcast_in_dim.18), calls=%async_computation.6 | async-start | bytes 1048576 | tf_op jit(solution)/shard_map/all_to_all | solution.py:11
  327.2 50.9 %all-to-all-start.9 = ((f32[32,1,256]{2,1,0:T(1,128)}), f32[32,1,256]{2,1,0:T(1,128)S(1)}, u32[]{:S(2)}, u32[]{:S(2)}) async-start(f32[32,1,256]{2,1,0:T(1,128)} %bitcast.27), calls=%async_computation.9 | async-start | bytes 65536 | tf_op jit(solution)/shard_map/all_to_all | solution.py:150
where the time goes:
time: 444 us; the launch traced here: 443 us
  local copies, waits for them, and re-layouts  149 us (34%)
  waiting for transfers between devices  119 us (27%)
  other arithmetic  85.4 us (19%)
  starting transfers between devices  48.7 us (11%)
  blocking collectives  30 us (7%)
  matrix products  9.72 us (2%)
    all_to_all x1, waiting for transfers between devices, per_device(): lax.all_to_all(found_rows, 'docs', split_axis=0, concat_axis=0, tiled=True)  92.7 us
    scatter-add x1, other arithmetic, per_device(): sstats = jnp.zeros((log_beta.shape[0], topic_cols), jnp.float32).at[own_r...  56.9 us
    gather x1, local copies, waits for them, and re-layouts, per_device(): found_rows = log_beta[request[0]]  33.6 us
    gather x1, local copies, waits for them, and re-layouts, per_device(): rescored = theta_all[source] + found_rows.astype(jnp.float32)  31.5 us
    all_to_all x1, blocking collectives, per_device(): lax.all_to_all(requests[0], 'docs', split_axis=0, concat_axis=0, tiled=True)  20.1 us
    all_to_all x4, starting transfers between devices, copy_for_each(): lax.all_to_all(jnp.broadcast_to(array[None], (devices, *array.shape)), ax...  17.7 us
    scatter x1, local copies, waits for them, and re-layouts, per_device(): blank_ids.at[places].set(counts.reshape(tokens)).reshape(owners, capacity)  16.1 us
    scatter x1, local copies, waits for them, and re-layouts, per_device(): norm_slots = jnp.zeros((owners * capacity,), jnp.float32).at[places].set(...  16.1 us
  transfers between devices with their start and end apart: 8, of which 5 were waited for; matrix products, arithmetic and copies ran while one was open for 22% of the time, Pallas kernels for 0%

commit v1 on v0

v1 whole, which is shorter than its diff:
```python
import functools

import jax
import jax.numpy as jnp
from jax import lax
from jax.experimental import pallas as pl
from jax.experimental.pallas import tpu as pltpu
from jax.sharding import PartitionSpec as P

ITERS = 3
LIFT = 30.0
BF, F32, I32 = jnp.bfloat16, jnp.float32, jnp.int32
NT = (((1,), (1,)), ((), ()))


def dot(a, b, dims=(((1,), (0,)), ((), ()))):
    return lax.dot_general(a, b, dims, preferred_element_type=F32)


def halves(x):
    high = x.astype(BF)
    return high, (x - high.astype(F32)).astype(BF)


def iota(shape, dim):
    return lax.broadcasted_iota(I32, shape, dim)


def line(ref, at, first):
    return jnp.concatenate([ref[at, first : first + 1, :], ref[at, first + 1 : first + 2, :]], axis=1)


def pack_kernel(block_ref, row_ref, count_ref, out_ref):
    docs, length = block_ref.shape
    owners = out_ref.shape[0]
    cap = 256
    earlier = (iota((length, length), 0) < iota((length, length), 1)).astype(BF)

    def step(d, carry):
        total, offset = carry
        owner, row, count = (ref[pl.ds(d, 1), :] for ref in (block_ref, row_ref, count_ref))
        owner = jnp.where(count > 0, owner, -1)
        member = (iota((owners, length), 0) == owner).astype(F32)
        before = dot(member.astype(BF), earlier) + offset
        rank = jnp.sum(member * before, axis=0, keepdims=True).astype(I32)
        place = (iota((cap, length), 0) == rank).astype(BF)
        values = jnp.concatenate(
            [
                member * (row % 128).astype(F32),
                member * (row // 128).astype(F32),
                member * (count * docs + d).astype(F32),
            ],
            axis=0,
        ).astype(BF)
        total = total + dot(values, place, NT)
        return total, offset + jnp.sum(member, axis=1, keepdims=True)

    total, offset = lax.fori_loop(
        0, docs, step, (jnp.zeros((3 * owners, cap), F32), jnp.zeros((owners, 1), F32))
    )
    row = (total[owners : 2 * owners] * 128 + total[:owners]).astype(I32)
    rest = total[2 * owners :].astype(I32)
    used = jnp.broadcast_to(offset, (owners, 128)).astype(I32)
    for half in range(2):
        lanes = slice(half * 128, half * 128 + 128)
        out_ref[:, half, :] = row[:, lanes]
        out_ref[:, 2 + half, :] = rest[:, lanes] % docs
        out_ref[:, 4 + half, :] = rest[:, lanes] // docs
        out_ref[:, 6 + half, :] = used


def fetch_kernel(req_ref, beta_ref, high_ref, low_ref, shift_ref, wide, raw):
    owners = req_ref.shape[0]
    chunk = 256

    def widen(i, _):
        at = pl.ds(i * chunk, chunk)
        wide[at, :] = beta_ref[at, :].astype(F32)
        return 0

    lax.fori_loop(0, beta_ref.shape[0] // chunk, widen, 0)

    def one(s, _):
        raw[...] = jnp.zeros(raw.shape, F32)

        def eight(j, _):
            for u in range(8):
                n = j * 8 + u
                r = req_ref[s, n // 128, n % 128]
                raw[pl.ds(j * 8 + u, 1), :] = wide[pl.ds(r, 1), :]
            return 0

        lax.fori_loop(0, pl.cdiv(req_ref[s, 6, 0], 8), eight, 0)
        x = raw[...]
        shift = jnp.max(x, axis=1, keepdims=True) - LIFT
        high, low = halves(jnp.exp(x - shift))
        high_ref[pl.ds(s * chunk, chunk), :] = high
        low_ref[pl.ds(s * chunk, chunk), :] = low
        diagonal = iota((chunk, chunk), 0) == iota((chunk, chunk), 1)
        shift_ref[pl.ds(s, 1), :] = jnp.sum(jnp.where(diagonal, shift, 0.0), axis=0, keepdims=True)
        return 0

    lax.fori_loop(0, owners, one, 0)


def mass_kernel(docs, req_ref, theta_ref, high_ref, low_ref, out_ref):
    def one(s, _):
        high, low = halves(theta_ref[pl.ds(s * docs, docs), :])
        at = pl.ds(s * 256, 256)
        both = dot(jnp.concatenate([high, low], axis=0), high_ref[at, :], NT)
        mass = both[:docs] + both[docs:] + dot(high, low_ref[at, :], NT)
        mine = iota((docs, 256), 0) == line(req_ref, s, 2)
        out_ref[pl.ds(s, 1), :] = jnp.sum(jnp.where(mine, mass, 0.0), axis=0, keepdims=True)
        return 0

    lax.fori_loop(0, req_ref.shape[0], one, 0)


def slot_weights(me, docs, req_ref, shift_ref, mass_ref, s):
    shift = shift_ref[:, s, :]
    scale = jnp.exp(shift - jnp.max(shift, axis=0, keepdims=True))
    norm = jnp.sum(scale * mass_ref[:, s, :], axis=0, keepdims=True)
    own = jnp.sum(jnp.where(iota(scale.shape, 0) == me, scale, 0.0), axis=0, keepdims=True)
    weight = line(req_ref, s, 4).astype(F32) * own / norm
    return jnp.where(iota((docs, 256), 0) == line(req_ref, s, 2), weight, 0.0)


def gather_kernel(docs, req_ref, shift_ref, mass_ref, high_ref, low_ref, out_ref):
    me = lax.axis_index("topics")

    def one(s, _):
        high, low = halves(slot_weights(me, docs, req_ref, shift_ref, mass_ref, s))
        at = pl.ds(s * 256, 256)
        both = dot(jnp.concatenate([high, low], axis=0), high_ref[at, :])
        out_ref[pl.ds(s * docs, docs), :] = both[:docs] + both[docs:] + dot(high, low_ref[at, :])
        return 0

    lax.fori_loop(0, req_ref.shape[0], one, 0)


def stats_kernel(docs, req_ref, row_ref, theta_ref, shift_ref, mass_ref, high_ref, low_ref, out_ref, terms):
    me = lax.axis_index("topics")

    def clear(i, _):
        out_ref[pl.ds(i * 256, 256), :] = jnp.zeros((256, out_ref.shape[1]), F32)
        return 0

    lax.fori_loop(0, out_ref.shape[0] // 256, clear, 0)

    def one(s, _):
        whigh, wlow = halves(slot_weights(me, docs, req_ref, shift_ref, mass_ref, s))
        thigh, tlow = halves(theta_ref[pl.ds(s * docs, docs), :])
        at = pl.ds(s * 256, 256)
        share = lax.dot_general(
            jnp.concatenate([whigh, whigh, wlow], axis=0),
            jnp.concatenate([thigh, tlow, thigh], axis=0),
            (((0,), (0,)), ((), ())),
            preferred_element_type=F32,
        )
        terms[...] = share * (high_ref[at, :].astype(F32) + low_ref[at, :].astype(F32))

        def eight(j, _):
            for u in range(8):
                n = j * 8 + u
                r = pl.ds(row_ref[s, n // 128, n % 128], 1)
                out_ref[r, :] = out_ref[r, :] + terms[pl.ds(j * 8 + u, 1), :]
            return 0

        lax.fori_loop(0, pl.cdiv(row_ref[s, 6, 0], 8), eight, 0)
        return 0

    lax.fori_loop(0, req_ref.shape[0], one, 0)


VM = pl.BlockSpec(memory_space=pltpu.VMEM)
SM = pl.BlockSpec(memory_space=pltpu.SMEM)


def call(kernel, outs, specs, scratch=()):
    many = isinstance(outs, (list, tuple))
    return pl.pallas_call(
        kernel,
        out_shape=outs,
        in_specs=specs,
        out_specs=[VM] * len(outs) if many else VM,
        scratch_shapes=list(scratch),
        compiler_params=pltpu.CompilerParams(vmem_limit_bytes=56 * 2**20),
    )


def shape(s, t=F32):
    return jax.ShapeDtypeStruct(s, t)


def to_all(x, axis):
    n = lax.axis_size(axis)
    return lax.all_to_all(jnp.broadcast_to(x[None], (n, *x.shape)), axis, 0, 0, tiled=True)


def per_device(log_beta, gamma_init, topic_prior, word_block, word_row, counts):
    docs, length = counts.shape
    words, cols = log_beta.shape
    owners = lax.axis_size("docs")
    slots = owners * 256
    request = call(pack_kernel, shape((owners, 8, 128), I32), [VM] * 3)(
        word_block[:, :, 0], word_row, counts
    )
    req = lax.all_to_all(request, "docs", 0, 0, tiled=True)
    high, low, shift = call(
        fetch_kernel,
        [shape((slots, cols), BF), shape((slots, cols), BF), shape((owners, 256))],
        [SM, VM],
        [pltpu.VMEM((words, cols), F32), pltpu.VMEM((256, cols), F32)],
    )(req, log_beta)
    shifts = to_all(shift, "topics")
    gamma = gamma_init
    for sweep in range(ITERS + 1):
        theta = jnp.exp(lax.digamma(gamma))
        thetas = to_all(theta, "docs").reshape(owners * docs, cols)
        mass = call(functools.partial(mass_kernel, docs), shape((owners, 256)), [VM] * 4)(
            req, thetas, high, low
        )
        masses = to_all(mass, "topics")
        if sweep < ITERS:
            part = call(functools.partial(gather_kernel, docs), shape((owners * docs, cols)), [VM] * 5)(
                req, shifts, masses, high, low
            )
            parts = lax.all_to_all(part.reshape(owners, docs, cols), "docs", 0, 0, tiled=True)
            gamma = topic_prior[None, :] + theta * jnp.sum(parts, axis=0)
    stats = call(
        functools.partial(stats_kernel, docs),
        shape((words, cols)),
        [VM, SM] + [VM] * 5,
        [pltpu.VMEM((256, cols), F32)],
    )(req, req, thetas, shifts, masses, high, low)
    return gamma, stats


def solution(mesh):
    return jax.shard_map(
        per_device,
        mesh=mesh,
        in_specs=(
            P("docs", "topics"),
            P("docs", "topics"),
            P("topics"),
            P("docs", None, None),
            P("docs", None),
            P("docs", None),
        ),
        out_specs=(P("docs", "topics"), P("docs", "topics")),
        check_vma=False,
    )
```

time: 444 us -> 438 us (0.986)
  the two profiles are of different devices: /device:TPU:2 before, /device:TPU:164 now
where the time goes in v1:
time: 438 us; the launch traced here: 437 us
  Pallas kernels  225 us (51%)
  blocking collectives  175 us (40%)
  starting transfers between devices  23.1 us (5%)
  local copies, waits for them, and re-layouts  6.96 us (2%)
    all_to_all x7, blocking collectives, to_all(): lax.all_to_all(jnp.broadcast_to(x[None], (n, *x.shape)), axis, 0, 0, tile...  109 us
    pallas_call x1, Pallas kernels, per_device(): call(functools.partial(stats_kernel, docs), shape((words, cols)), [VM, SM...  74.1 us
    pallas_call x1, Pallas kernels, per_device(): call(fetch_kernel, [shape((slots, cols), BF), shape((slots, cols), BF), s...  69.9 us
    all_to_all x3, blocking collectives, per_device(): lax.all_to_all(part.reshape(owners, docs, cols), 'docs', 0, 0, tiled=True)  65.6 us
    pallas_call x4, Pallas kernels, per_device(): call(functools.partial(mass_kernel, docs), shape((owners, 256)), [VM] * 4)  42.9 us
    pallas_call x3, Pallas kernels, per_device(): call(functools.partial(gather_kernel, docs), shape((owners * docs, cols))...  30.3 us
    all_to_all x2, starting transfers between devices, to_all(): lax.all_to_all(jnp.broadcast_to(x[None], (n, *x.shape)), axis, 0, 0, tile...  13.8 us
    all_to_all x1, starting transfers between devices, per_device(): req = lax.all_to_all(request, 'docs', 0, 0, tiled=True)  9.34 us
  transfers between devices with their start and end apart: 3, of which 1 were waited for; matrix products, arithmetic and copies ran while one was open for 0% of the time, Pallas kernels for 18%

profile of v1, /device:TPU:164, one launch (start us, length us, event | category | flops | bytes accessed | tf_op | source)
XLA Modules:
  0.0 436.7 jit_solution(8759132183222036084)
XLA Ops:
  2.0 7.5 %shard_map.77 = s32[32,8,128]{2,1,0:T(8,128)} custom-call(s32[16,256]{1,0:T(8,128)} %bitcast.18, s32[16,256]{1,0:T(8,128)} %row_ref.1, s32[16,256]{1,0:T(8,128)} %count_ref.1), custom_call_target="tpu_custom_call" | custom-call | tf_op jit(solution)/shard_map/pallas_call | solution.py:205
  9.5 9.3 %all-to-all-start = ((s32[32,8,128]{2,1,0:T(8,128)}), s32[32,8,128]{2,1,0:T(8,128)S(1)}, u32[]{:S(2)}, u32[]{:S(2)}) async-start(s32[32,8,128]{2,1,0:T(8,128)} %shard_map.77), calls=%async_computation | async-start | bytes 262144 | tf_op jit(solution)/shard_map/all_to_all | solution.py:208
  19.7 4.0 all-to-all-done.req_ref.row_ref
  24.5 9.3 %all-to-all-start.2 = ((f32[32,16,256]{2,1,0:T(8,128)}), f32[32,16,256]{2,1,0:T(8,128)S(1)}, u32[]{:S(2)}, u32[]{:S(2)}) async-start(f32[32,16,256]{2,1,0:T(8,128)} %broadcast_in_dim.19), calls=%async_computation.2 | async-start | bytes 1048576 | tf_op jit(solution)/shard_map/all_to_all | solution.py:197
  33.9 69.9 %shard_map.78 = (bf16[8192,256]{1,0:T(8,128)(2,1)}, bf16[8192,256]{1,0:T(8,128)(2,1)}, f32[32,256]{1,0:T(8,128)}) custom-call(s32[32,8,128]{2,1,0:T(8,128)} %copy-done, bf16[8192,256]{1,0:T(8,128)(2,1)} %beta_ref.1), custom_call_target="tpu_custom_call" | custom-call | tf_op jit(solution)/shard_map/pallas_call | solution.py:209
  105.2 4.5 %all-to-all-start.1 = ((f32[8,32,256]{2,1,0:T(8,128)}), f32[8,32,256]{2,1,0:T(8,128)S(1)}, u32[]{:S(2)}, u32[]{:S(2)}) async-start(f32[8,32,256]{2,1,0:T(8,128)} %broadcast_in_dim.18), calls=%async_computation.1 | async-start | bytes 524288 | tf_op jit(solution)/shard_map/all_to_all | solution.py:197
  109.7 10.7 %shard_map.79 = f32[32,256]{1,0:T(8,128)} custom-call(s32[32,8,128]{2,1,0:T(8,128)} %copy-done, f32[512,256]{1,0:T(8,128)} %bitcast.12, bf16[8192,256]{1,0:T(8,128)(2,1)} %get-tuple-element.6.high_ref, bf16[8192,256]{1,0:T(8,128)(2,1)} %get-tuple-element.7.low_ref), custom_call_target="tpu_custom_call" | custom-call | tf_op jit(solution)/shard_map/pallas_call | solution.py:220
  121.2 12.2 %all_to_all.65.mass_ref = f32[8,32,256]{2,1,0:T(8,128)} all-to-all(f32[8,32,256]{2,1,0:T(8,128)S(1)} %broadcast_in_dim.20), channel_id=1, replica_groups=mesh['docs'=32,'topics'=8] {'topics'}, dimensions={0} | all-to-all | bytes 524288 | tf_op jit(solution)/shard_map/all_to_all | solution.py:197
  133.5 10.1 %shard_map.80 = f32[512,256]{1,0:T(8,128)} custom-call(s32[32,8,128]{2,1,0:T(8,128)} %copy-done, f32[8,32,256]{2,1,0:T(8,128)} %copy-done.1, f32[8,32,256]{2,1,0:T(8,128)} %all_to_all.65.mass_ref, bf16[8192,256]{1,0:T(8,128)(2,1)} %get-tuple-element.6.high_ref, bf16[8192,256]{1,0:T(8,128)(2,1)} %get-tuple-element.7.low_ref), custom_call_target="tpu_custom_call" | custom-call | tf_op jit(solution)/shard_map/pallas_call | solution.py:225
  143.6 21.4 %all_to_all.66 = f32[32,16,256]{2,1,0:T(8,128)S(1)} all-to-all(f32[32,16,256]{2,1,0:T(8,128)} %bitcast.13), channel_id=1, replica_groups=mesh['docs'=32,'topics'=8] {'docs'}, dimensions={0} | all-to-all | bytes 1048576 | tf_op jit(solution)/shard_map/all_to_all | solution.py:228
  165.4 21.8 %all_to_all.67 = f32[32,16,256]{2,1,0:T(8,128)} all-to-all(f32[32,16,256]{2,1,0:T(8,128)S(1)} %broadcast_in_dim.21), channel_id=1, replica_groups=mesh['docs'=32,'topics'=8] {'docs'}, dimensions={0} | all-to-all | bytes 1048576 | tf_op jit(solution)/shard_map/all_to_all | solution.py:197
  187.2 10.7 %shard_map.81 = f32[32,256]{1,0:T(8,128)} custom-call(s32[32,8,128]{2,1,0:T(8,128)} %copy-done, f32[512,256]{1,0:T(8,128)} %bitcast.14, bf16[8192,256]{1,0:T(8,128)(2,1)} %get-tuple-element.6.high_ref, bf16[8192,256]{1,0:T(8,128)(2,1)} %get-tuple-element.7.low_ref), custom_call_target="tpu_custom_call" | custom-call | tf_op jit(solution)/shard_map/pallas_call | solution.py:220
  198.8 10.6 %all_to_all.68.mass_ref = f32[8,32,256]{2,1,0:T(8,128)} all-to-all(f32[8,32,256]{2,1,0:T(8,128)S(1)} %broadcast_in_dim.22), channel_id=1, replica_groups=mesh['docs'=32,'topics'=8] {'topics'}, dimensions={0} | all-to-all | bytes 524288 | tf_op jit(solution)/shard_map/all_to_all | solution.py:197
  209.3 10.1 %shard_map.82 = f32[512,256]{1,0:T(8,128)} custom-call(s32[32,8,128]{2,1,0:T(8,128)} %copy-done, f32[8,32,256]{2,1,0:T(8,128)} %copy-done.1, f32[8,32,256]{2,1,0:T(8,128)} %all_to_all.68.mass_ref, bf16[8192,256]{1,0:T(8,128)(2,1)} %get-tuple-element.6.high_ref, bf16[8192,256]{1,0:T(8,128)(2,1)} %get-tuple-element.7.low_ref), custom_call_target="tpu_custom_call" | custom-call | tf_op jit(solution)/shard_map/pallas_call | solution.py:225
  219.4 22.1 %all_to_all.69 = f32[32,16,256]{2,1,0:T(8,128)S(1)} all-to-all(f32[32,16,256]{2,1,0:T(8,128)} %bitcast.15), channel_id=1, replica_groups=mesh['docs'=32,'topics'=8] {'docs'}, dimensions={0} | all-to-all | bytes 1048576 | tf_op jit(solution)/shard_map/all_to_all | solution.py:228
  241.8 21.8 %all_to_all.70 = f32[32,16,256]{2,1,0:T(8,128)} all-to-all(f32[32,16,256]{2,1,0:T(8,128)S(1)} %broadcast_in_dim.23), channel_id=1, replica_groups=mesh['docs'=32,'topics'=8] {'docs'}, dimensions={0} | all-to-all | bytes 1048576 | tf_op jit(solution)/shard_map/all_to_all | solution.py:197
  263.6 10.7 %shard_map.83 = f32[32,256]{1,0:T(8,128)} custom-call(s32[32,8,128]{2,1,0:T(8,128)} %copy-done, f32[512,256]{1,0:T(8,128)} %bitcast.16, bf16[8192,256]{1,0:T(8,128)(2,1)} %get-tuple-element.6.high_ref, bf16[8192,256]{1,0:T(8,128)(2,1)} %get-tuple-element.7.low_ref), custom_call_target="tpu_custom_call" | custom-call | tf_op jit(solution)/shard_map/pallas_call | solution.py:220
  275.1 10.6 %all_to_all.71.mass_ref = f32[8,32,256]{2,1,0:T(8,128)} all-to-all(f32[8,32,256]{2,1,0:T(8,128)S(1)} %broadcast_in_dim.24), channel_id=1, replica_groups=mesh['docs'=32,'topics'=8] {'topics'}, dimensions={0} | all-to-all | bytes 524288 | tf_op jit(solution)/shard_map/all_to_all | solution.py:197
  285.7 10.1 %shard_map.84 = f32[512,256]{1,0:T(8,128)} custom-call(s32[32,8,128]{2,1,0:T(8,128)} %copy-done, f32[8,32,256]{2,1,0:T(8,128)} %copy-done.1, f32[8,32,256]{2,1,0:T(8,128)} %all_to_all.71.mass_ref, bf16[8192,256]{1,0:T(8,128)(2,1)} %get-tuple-element.6.high_ref, bf16[8192,256]{1,0:T(8,128)(2,1)} %get-tuple-element.7.low_ref), custom_call_target="tpu_custom_call" | custom-call | tf_op jit(solution)/shard_map/pallas_call | solution.py:225
  295.8 22.1 %all_to_all.72 = f32[32,16,256]{2,1,0:T(8,128)S(1)} all-to-all(f32[32,16,256]{2,1,0:T(8,128)} %bitcast.17), channel_id=1, replica_groups=mesh['docs'=32,'topics'=8] {'docs'}, dimensions={0} | all-to-all | bytes 1048576 | tf_op jit(solution)/shard_map/all_to_all | solution.py:228
  318.6 21.8 %all_to_all.73 = f32[32,16,256]{2,1,0:T(8,128)} all-to-all(f32[32,16,256]{2,1,0:T(8,128)S(1)} %broadcast_in_dim.25), channel_id=1, replica_groups=mesh['docs'=32,'topics'=8] {'docs'}, dimensions={0} | all-to-all | bytes 1048576 | tf_op jit(solution)/shard_map/all_to_all | solution.py:197
  340.5 10.7 %shard_map.85 = f32[32,256]{1,0:T(8,128)} custom-call(s32[32,8,128]{2,1,0:T(8,128)} %copy-done, f32[512,256]{1,0:T(8,128)} %bitcast.10, bf16[8192,256]{1,0:T(8,128)(2,1)} %get-tuple-element.6.high_ref, bf16[8192,256]{1,0:T(8,128)(2,1)} %get-tuple-element.7.low_ref), custom_call_target="tpu_custom_call" | custom-call | tf_op jit(solution)/shard_map/pallas_call | solution.py:220
  352.0 10.6 %all_to_all.74.mass_ref = f32[8,32,256]{2,1,0:T(8,128)} all-to-all(f32[8,32,256]{2,1,0:T(8,128)S(1)} %broadcast_in_dim.26), channel_id=1, replica_groups=mesh['docs'=32,'topics'=8] {'topics'}, dimensions={0} | all-to-all | bytes 524288 | tf_op jit(solution)/shard_map/all_to_all | solution.py:197
  362.6 74.1 %shard_map.86 = f32[8192,256]{1,0:T(8,128)} custom-call(s32[32,8,128]{2,1,0:T(8,128)} %copy-done, s32[32,8,128]{2,1,0:T(8,128)} %copy-done, f32[512,256]{1,0:T(8,128)} %bitcast.11, f32[8,32,256]{2,1,0:T(8,128)} %copy-done.1, f32[8,32,256]{2,1,0:T(8,128)} %all_to_all.74.mass_ref, bf16[8192,256]{1,0:T(8,128)(2,1)} %get-tuple-element.6.high_ref, ...), custom_call_target="tpu_custom_call" | custom-call | tf_op jit(solution)/shard_map/pallas_call | solution.py:230
  (29 shorter events, 9.0 us)
Async XLA Ops:
  9.5 14.2 %all-to-all-start = ((s32[32,8,128]{2,1,0:T(8,128)}), s32[32,8,128]{2,1,0:T(8,128)S(1)}, u32[]{:S(2)}, u32[]{:S(2)}) async-start(s32[32,8,128]{2,1,0:T(8,128)} %shard_map.77), calls=%async_computation | async-start | bytes 262144 | tf_op jit(solution)/shard_map/all_to_all | solution.py:208
  23.7 10.2 %copy-start = (s32[32,8,128]{2,1,0:T(8,128)}, s32[32,8,128]{2,1,0:T(8,128)S(1)}, u32[]{:S(2)}) copy-start(s32[32,8,128]{2,1,0:T(8,128)S(1)} %all-to-all-done.req_ref.row_ref) | copy-start | bytes 393220
  24.5 79.2 %all-to-all-start.2 = ((f32[32,16,256]{2,1,0:T(8,128)}), f32[32,16,256]{2,1,0:T(8,128)S(1)}, u32[]{:S(2)}, u32[]{:S(2)}) async-start(f32[32,16,256]{2,1,0:T(8,128)} %broadcast_in_dim.19), calls=%async_computation.2 | async-start | bytes 1048576 | tf_op jit(solution)/shard_map/all_to_all | solution.py:197
  103.7 6.0 %copy-start.2 = (f32[32,16,256]{2,1,0:T(8,128)}, f32[32,16,256]{2,1,0:T(8,128)S(1)}, u32[]{:S(2)}) copy-start(f32[32,16,256]{2,1,0:T(8,128)S(1)} %all-to-all-done.2) | copy-start | bytes 1572868
  105.2 15.2 %all-to-all-start.1 = ((f32[8,32,256]{2,1,0:T(8,128)}), f32[8,32,256]{2,1,0:T(8,128)S(1)}, u32[]{:S(2)}, u32[]{:S(2)}) async-start(f32[8,32,256]{2,1,0:T(8,128)} %broadcast_in_dim.18), calls=%async_computation.1 | async-start | bytes 524288 | tf_op jit(solution)/shard_map/all_to_all | solution.py:197
  120.5 13.0 %copy-start.1 = (f32[8,32,256]{2,1,0:T(8,128)}, f32[8,32,256]{2,1,0:T(8,128)S(1)}, u32[]{:S(2)}) copy-start(f32[8,32,256]{2,1,0:T(8,128)S(1)} %all-to-all-done.1.shift_ref) | copy-start | bytes 786436
  133.5 31.6 %copy-start.3 = (f32[16,256]{1,0:T(8,128)S(1)}, f32[16,256]{1,0:T(8,128)}, u32[]{:S(2)}) copy-start(f32[16,256]{1,0:T(8,128)} %param.7) | copy-start | bytes 49156
  133.5 31.6 %copy-start.4 = (f32[256]{0:T(256)S(1)}, f32[256]{0:T(256)}, u32[]{:S(2)}) copy-start(f32[256]{0:T(256)} %param.8) | copy-start | bytes 3076

commit v2 on v1

v2 whole, which is shorter than its diff:
```python
import functools

import jax
import jax.numpy as jnp
from jax import lax
from jax.experimental import pallas as pl
from jax.experimental.pallas import tpu as pltpu
from jax.sharding import PartitionSpec as P

ITERS = 3
LIFT = 30.0
BF, F32, I32 = jnp.bfloat16, jnp.float32, jnp.int32
NN = (((1,), (0,)), ((), ()))
NT = (((1,), (1,)), ((), ()))
TN = (((0,), (0,)), ((), ()))
MESH = pl.DeviceIdType.MESH
CAP = 256


def dot(a, b, dims=NN):
    return lax.dot_general(a, b, dims, preferred_element_type=F32)


def halves(x):
    high = x.astype(BF)
    return high, (x - high.astype(F32)).astype(BF)


def iota(shape, dim):
    return lax.broadcasted_iota(I32, shape, dim)


def grid_of(owners):
    return {32: 8}.get(owners, owners // 2)


def pack_kernel(block_ref, row_ref, count_ref, out_ref):
    docs, length = block_ref.shape
    owners = out_ref.shape[0]
    earlier = (iota((length, length), 0) < iota((length, length), 1)).astype(BF)

    def step(d, carry):
        total, offset = carry
        owner, row, count = (ref[pl.ds(d, 1), :] for ref in (block_ref, row_ref, count_ref))
        owner = jnp.where(count > 0, owner, -1)
        member = (iota((owners, length), 0) == owner).astype(F32)
        before = dot(member.astype(BF), earlier) + offset
        rank = jnp.sum(member * before, axis=0, keepdims=True).astype(I32)
        place = (iota((CAP, length), 0) == rank).astype(BF)
        values = jnp.concatenate(
            [
                member * (row % 128).astype(F32),
                member * (row // 128).astype(F32),
                member * (count * docs + d).astype(F32),
            ],
            axis=0,
        ).astype(BF)
        total = total + dot(values, place, NT)
        return total, offset + jnp.sum(member, axis=1, keepdims=True)

    total, offset = lax.fori_loop(
        0, docs, step, (jnp.zeros((3 * owners, CAP), F32), jnp.zeros((owners, 1), F32))
    )
    row = (total[owners : 2 * owners] * 128 + total[:owners]).astype(I32)
    rest = total[2 * owners :].astype(I32)
    used = jnp.broadcast_to(offset, (owners, 128)).astype(I32)
    for half in range(2):
        lanes = slice(half * 128, half * 128 + 128)
        out_ref[:, half, :] = row[:, lanes]
        out_ref[:, 2 + half, :] = rest[:, lanes] % docs
        out_ref[:, 4 + half, :] = rest[:, lanes] // docs
        out_ref[:, 6 + half, :] = used


def fetch_kernel(rows_ref, used_ref, beta_ref, high_ref, low_ref, shift_ref, wide, raw):
    owners = used_ref.shape[0]

    def widen(i, _):
        at = pl.ds(pl.multiple_of(i * CAP, CAP), CAP)
        wide[at, :] = beta_ref[at, :].astype(F32)
        return 0

    lax.fori_loop(0, beta_ref.shape[0] // CAP, widen, 0)
    raw[...] = jnp.zeros(raw.shape, F32)
    first = (iota((8, 128), 1) == 0).astype(BF)

    def one(s, _):
        def eight(j, _):
            to = raw.at[pl.ds(pl.multiple_of(j * 8, 8), 8), :]
            base = s * CAP + j * 8
            values = [wide[pl.ds(rows_ref[base + u], 1), :] for u in range(8)]
            for u in range(8):
                to[u : u + 1, :] = values[u]
            return 0

        lax.fori_loop(0, (used_ref[s] + 7) >> 3, eight, 0)
        x = raw[...]
        top = jnp.max(x, axis=1, keepdims=True)
        high, low = halves(jnp.exp(x - (top - LIFT)))
        at = pl.ds(pl.multiple_of(s * CAP, CAP), CAP)
        high_ref[at, :] = high
        low_ref[at, :] = low
        tops = dot(first, jnp.broadcast_to(top, (CAP, 128)).astype(BF), NT)
        shift_ref[pl.ds(s, 1), :] = tops[:1] - LIFT
        return 0

    lax.fori_loop(0, owners, one, 0)


def exp_digamma(g):
    z = g + 6.0
    total = 1.0 / g
    for i in range(1, 6):
        total = total + 1.0 / (g + float(i))
    inverse = 1.0 / z
    square = inverse * inverse
    series = square * (1 / 12 - square * (1 / 120 - square * (1 / 252 - square * (1 / 240))))
    return jnp.exp(jnp.log(z) - 0.5 * inverse - series - total)


def sweeps_kernel(
    nx, nz, groups,
    req_ref, gamma_ref, prior_ref, shift_ref, high_hbm, low_hbm,
    gamma_out, theta_out, weight_out,
    high_ref, low_ref, theta, own_theta, scales, masses, counts, holders, weights, parts, xparts, zbase, zparts,
    load_sem, shift_send, shift_recv, mass_send, mass_recv, tz_send, tz_recv, tx_send, tx_recv, sx_send, sx_recv, sz_send, sz_recv,
):
    owners = nx * nz
    docs = gamma_ref.shape[0]
    me, top = lax.axis_index("docs"), lax.axis_index("topics")
    x, z = me // nz, me % nz

    def at_x(d):
        return (x + d) % nx

    def at_z(d):
        return (z + d) % nz

    def block(i):
        return pl.ds(pl.multiple_of(i * docs, docs), docs)

    def remote(src, dst, send, recv, **device):
        return pltpu.make_async_remote_copy(
            src_ref=src, dst_ref=dst, send_sem=send, recv_sem=recv, device_id=device, device_id_type=MESH
        )

    barrier = pltpu.get_barrier_semaphore()
    for d in range(1, nz):
        pl.semaphore_signal(barrier, inc=1, device_id={"docs": x * nz + at_z(d)}, device_id_type=MESH)
    for d in range(1, nx):
        pl.semaphore_signal(barrier, inc=1, device_id={"docs": at_x(d) * nz + z}, device_id_type=MESH)
    for d in range(1, groups):
        pl.semaphore_signal(barrier, inc=1, device_id={"topics": (top + d) % groups}, device_id_type=MESH)
    loads = [
        pltpu.make_async_copy(high_hbm, high_ref, load_sem.at[0]),
        pltpu.make_async_copy(low_hbm, low_ref, load_sem.at[1]),
    ]
    for copy in loads:
        copy.start()
    counts[...] = jnp.concatenate([req_ref[:, 4, :], req_ref[:, 5, :]], axis=1).astype(F32)
    holders[...] = jnp.concatenate([req_ref[:, 2, :], req_ref[:, 3, :]], axis=1)
    gamma_out[...] = gamma_ref[...]
    first = exp_digamma(gamma_ref[...])
    own_theta[...] = first
    theta[block(me), :] = first
    scales[top] = shift_ref[...]
    pl.semaphore_wait(barrier, nz - 1 + nx - 1 + groups - 1)

    def shift_copy(d):
        return remote(shift_ref, scales.at[top], shift_send.at[d], shift_recv.at[d], topics=(top + d) % groups)

    for d in range(1, groups):
        shift_copy(d).start()

    def turn(k):
        return jnp.where(k % 2 == 1, (k + 1) // 2, (nz - k // 2) % nz)

    def tz_copy(d):
        return remote(theta.at[block(me)], theta.at[block(me)], tz_send.at[d], tz_recv.at[d], docs=x * nz + at_z(d))

    def tx_copy(dx, dz):
        b = block(x * nz + at_z(nz - dz))
        return remote(theta.at[b], theta.at[b], tx_send.at[dx, dz], tx_recv.at[dx, dz], docs=at_x(dx) * nz + z)

    def sx_copy(dx, dz):
        b = block(at_x(dx) * nz + at_z(dz))
        return remote(parts.at[b], xparts.at[dx, dz], sx_send.at[dx, dz], sx_recv.at[dx, dz], docs=at_x(dx) * nz + z)

    def sz_copy(d):
        return remote(zbase.at[d], zparts.at[d], sz_send.at[d], sz_recv.at[d], docs=x * nz + at_z(d))

    def mass_of(p, s):
        high, low = halves(theta[block(s), :])
        at = pl.ds(pl.multiple_of(s * CAP, CAP), CAP)
        both = dot(jnp.concatenate([high, low], axis=0), high_ref[at, :], NT)
        mass = both[:docs] + both[docs:] + dot(high, low_ref[at, :], NT)
        mine = iota((docs, CAP), 0) == holders[pl.ds(s, 1), :]
        masses[p, top, pl.ds(s, 1), :] = jnp.sum(jnp.where(mine, mass, 0.0), axis=0, keepdims=True)

    def masses_of(p, wait_loads):
        for d in range(1, nz):
            tz_copy(d).start()
        for d in range(1, nx):
            tx_copy(d, 0).start()
        if wait_loads:
            for copy in loads:
                copy.wait()
        mass_of(p, me)

        def column(k, _):
            dz = turn(k)
            tz_copy(dz).wait_recv()
            for d in range(1, nx):
                tx_copy(d, dz).start()
            mass_of(p, x * nz + at_z(nz - dz))
            return 0

        lax.fori_loop(1, nz, column, 0)

        def rest(k, _):
            dz = turn(k)
            for d in range(1, nx):
                tx_copy(d, dz).wait_recv()
            for d in range(1, nx):
                mass_of(p, at_x(nx - d) * nz + at_z(nz - dz))
            return 0

        lax.fori_loop(0, nz, rest, 0)

        def mass_copy(d):
            return remote(
                masses.at[p, top], masses.at[p, top], mass_send.at[d], mass_recv.at[p, d], topics=(top + d) % groups
            )

        for d in range(1, groups):
            mass_copy(d).start()
        for d in range(1, nz):
            tz_copy(d).wait_send()

        def sent(k, _):
            for d in range(1, nx):
                tx_copy(d, k).wait_send()
            return 0

        lax.fori_loop(0, nz, sent, 0)
        for d in range(1, groups):
            mass_copy(d).wait()
        if wait_loads:
            for d in range(1, groups):
                shift_copy(d).wait()
            peak = scales[0]
            for t in range(1, groups):
                peak = jnp.maximum(peak, scales[t])
            for t in range(groups):
                scales[t] = jnp.exp(scales[t] - peak)
        norm = scales[0] * masses[p, 0]
        for t in range(1, groups):
            norm = norm + scales[t] * masses[p, t]
        weights[...] = counts[...] * scales[top] / norm

    def part_of(s):
        mine = iota((docs, CAP), 0) == holders[pl.ds(s, 1), :]
        high, low = halves(jnp.where(mine, weights[pl.ds(s, 1), :], 0.0))
        at = pl.ds(pl.multiple_of(s * CAP, CAP), CAP)
        both = dot(jnp.concatenate([high, low], axis=0), high_ref[at, :])
        parts[block(s), :] = both[:docs] + both[docs:] + dot(high, low_ref[at, :])

    def renew():
        def scatter(k, _):
            dz = turn(nz - 1 - k)
            for d in range(nx):
                part_of(at_x(d) * nz + at_z(dz))
            for d in range(1, nx):
                sx_copy(d, dz).start()
            return 0

        lax.fori_loop(0, nz, scatter, 0)

        def joined(dz):
            total = parts[block(x * nz + at_z(dz)), :]
            for d in range(1, nx):
                sx_copy(d, dz).wait_recv()
                total = total + xparts[d, dz]
            return total

        def onward(k, _):
            dz = turn(nz - 1 - k)
            zbase[dz] = joined(dz)
            sz_copy(dz).start()
            return 0

        lax.fori_loop(0, nz - 1, onward, 0)
        total = joined(0)
        for d in range(1, nz):
            sz_copy(d).wait_recv()
            total = total + zparts[d]
        gamma = prior_ref[...] + own_theta[...] * total
        gamma_out[...] = gamma
        new = exp_digamma(gamma)
        own_theta[...] = new
        theta[block(me), :] = new
        for d in range(1, nz):
            sz_copy(d).wait_send()

        def sent(k, _):
            for d in range(1, nx):
                sx_copy(d, k).wait_send()
            return 0

        lax.fori_loop(0, nz, sent, 0)

    masses_of(0, True)
    renew()

    def sweep(i, _):
        masses_of(i % 2, False)
        renew()
        return 0

    lax.fori_loop(1, ITERS, sweep, 0)
    masses_of(ITERS % 2, False)
    weight_out[...] = weights[...]
    theta_out[...] = theta[...]


def stats_kernel(docs, rows_ref, used_ref, req_ref, theta_ref, weight_ref, high_ref, low_ref, out_ref, terms, *more):
    sums = (out_ref, *more)

    def clear(i, _):
        for total in sums:
            total[pl.ds(pl.multiple_of(i * CAP, CAP), CAP), :] = jnp.zeros((CAP, out_ref.shape[1]), F32)
        return 0

    lax.fori_loop(0, out_ref.shape[0] // CAP, clear, 0)

    def one(s, _):
        holder = jnp.concatenate([req_ref[s, 2:3, :], req_ref[s, 3:4, :]], axis=1)
        weight = jnp.where(iota((docs, CAP), 0) == holder, weight_ref[pl.ds(s, 1), :], 0.0)
        whigh, wlow = halves(weight)
        thigh, tlow = halves(theta_ref[pl.ds(pl.multiple_of(s * docs, docs), docs), :])
        at = pl.ds(pl.multiple_of(s * CAP, CAP), CAP)
        share = dot(
            jnp.concatenate([whigh, whigh, wlow], axis=0), jnp.concatenate([thigh, tlow, thigh], axis=0), TN
        )
        terms[...] = share * (high_ref[at, :].astype(F32) + low_ref[at, :].astype(F32))

        def eight(j, _):
            base = s * CAP + j * 8
            now = terms.at[pl.ds(pl.multiple_of(j * 8, 8), 8), :]
            rows = [rows_ref[base + u] for u in range(8)]
            for start in range(0, 8, len(sums)):
                news = []
                for k, total in enumerate(sums):
                    u = start + k
                    news.append(total[pl.ds(rows[u], 1), :] + now[u : u + 1, :])
                for k, total in enumerate(sums):
                    total[pl.ds(rows[start + k], 1), :] = news[k]
            return 0

        lax.fori_loop(0, (used_ref[s] + 7) >> 3, eight, 0)
        return 0

    lax.fori_loop(0, used_ref.shape[0], one, 0)

    def finish(i, _):
        at = pl.ds(pl.multiple_of(i * CAP, CAP), CAP)
        out_ref[at, :] = functools.reduce(jnp.add, [total[at, :] for total in sums])
        return 0

    lax.fori_loop(0, out_ref.shape[0] // CAP, finish, 0)


VM = pl.BlockSpec(memory_space=pltpu.VMEM)
SM = pl.BlockSpec(memory_space=pltpu.SMEM)
AN = pl.BlockSpec(memory_space=pl.ANY)


def call(kernel, outs, specs, scratch=(), **params):
    many = isinstance(outs, (list, tuple))
    return pl.pallas_call(
        kernel,
        out_shape=outs,
        in_specs=specs,
        out_specs=[VM] * len(outs) if many else VM,
        scratch_shapes=list(scratch),
        compiler_params=pltpu.CompilerParams(vmem_limit_bytes=60 * 2**20, **params),
    )


def shape(s, t=F32):
    return jax.ShapeDtypeStruct(s, t)


def per_device(log_beta, gamma_init, topic_prior, word_block, word_row, counts):
    docs, length = counts.shape
    words, cols = log_beta.shape
    owners, groups = lax.axis_size("docs"), lax.axis_size("topics")
    nz = grid_of(owners)
    nx = owners // nz
    slots = owners * CAP
    request = call(pack_kernel, shape((owners, 8, 128), I32), [VM] * 3)(
        word_block[:, :, 0], word_row, counts
    )
    req = lax.all_to_all(request, "docs", 0, 0, tiled=True)
    rows, used = req[:, :2, :].reshape(slots), req[:, 6, 0]
    high, low, shift = call(
        fetch_kernel,
        [shape((slots, cols), BF), shape((slots, cols), BF), shape((owners, CAP))],
        [SM, SM, VM],
        [pltpu.VMEM((words, cols), F32), pltpu.VMEM((CAP, cols), F32)],
    )(rows, used, log_beta)
    D = pltpu.SemaphoreType.DMA
    block = (docs, cols)
    gamma, theta, weight = call(
        functools.partial(sweeps_kernel, nx, nz, groups),
        [shape(block), shape((owners * docs, cols)), shape((owners, CAP))],
        [VM] * 4 + [AN] * 2,
        [
            pltpu.VMEM((slots, cols), BF),
            pltpu.VMEM((slots, cols), BF),
            pltpu.VMEM((owners * docs, cols), F32),
            pltpu.VMEM(block, F32),
            pltpu.VMEM((groups, owners, CAP), F32),
            pltpu.VMEM((2, groups, owners, CAP), F32),
            pltpu.VMEM((owners, CAP), F32),
            pltpu.VMEM((owners, CAP), I32),
            pltpu.VMEM((owners, CAP), F32),
            pltpu.VMEM((owners * docs, cols), F32),
            pltpu.VMEM((nx, nz, *block), F32),
            pltpu.VMEM((nz, *block), F32),
            pltpu.VMEM((nz, *block), F32),
            D((2,)), D((groups,)), D((groups,)), D((groups,)), D((2, groups)),
            D((nz,)), D((nz,)), D((nx, nz)), D((nx, nz)), D((nx, nz)), D((nx, nz)), D((nz,)), D((nz,)),
        ],
        collective_id=1,
        has_side_effects=True,
    )(req, gamma_init, topic_prior[None, :], shift, high, low)
    stats = call(
        functools.partial(stats_kernel, docs),
        shape((words, cols)),
        [SM, SM] + [VM] * 5,
        [pltpu.VMEM((CAP, cols), F32)] + [pltpu.VMEM((words, cols), F32)] * 3,
    )(rows, used, req, theta, weight, high, low)
    return gamma, stats


def solution(mesh):
    return jax.shard_map(
        per_device,
        mesh=mesh,
        in_specs=(
            P("docs", "topics"),
            P("docs", "topics"),
            P("topics"),
            P("docs", None, None),
            P("docs", None),
            P("docs", None),
        ),
        out_specs=(P("docs", "topics"), P("docs", "topics")),
        check_vma=False,
    )
```

time: 438 us -> 190 us (0.43)
  the two profiles are of different devices: /device:TPU:164 before, /device:TPU:167 now
where the time goes in v2:
time: 190 us; the launch traced here: 188 us
  Pallas kernels  170 us (89%)
  blocking collectives  13.1 us (7%)
  local copies, waits for them, and re-layouts  3.78 us (2%)
    pallas_call x1, Pallas kernels, per_device(): call(functools.partial(sweeps_kernel, nx, nz, groups), [shape(block), sha...  103 us
    pallas_call x1, Pallas kernels, per_device(): call(functools.partial(stats_kernel, docs), shape((words, cols)), [SM, SM...  31.7 us
    pallas_call x1, Pallas kernels, per_device(): call(fetch_kernel, [shape((slots, cols), BF), shape((slots, cols), BF), s...  28.3 us
    all_to_all x1, blocking collectives, per_device(): req = lax.all_to_all(request, 'docs', 0, 0, tiled=True)  13.1 us
    pallas_call x1, Pallas kernels, per_device(): call(pack_kernel, shape((owners, 8, 128), I32), [VM] * 3)  7.53 us

profile of v2, /device:TPU:167, one launch (start us, length us, event | category | flops | bytes accessed | tf_op | source)
XLA Modules:
  0.0 187.6 jit_solution(15930463216638444855)
XLA Ops:
  0.6 1.3 copy.10
  2.0 7.5 %shard_map.77 = s32[32,8,128]{2,1,0:T(8,128)} custom-call(s32[16,256]{1,0:T(8,128)} %bitcast.7, s32[16,256]{1,0:T(8,128)} %row_ref.1, s32[16,256]{1,0:T(8,128)} %count_ref.1), custom_call_target="tpu_custom_call" | custom-call | tf_op jit(solution)/shard_map/pallas_call | solution.py:401
  9.5 13.1 %all_to_all.5.req_ref = s32[32,8,128]{2,1,0:T(8,128)S(1)} all-to-all(s32[32,8,128]{2,1,0:T(8,128)} %shard_map.77), channel_id=1, replica_groups=mesh['docs'=32,'topics'=8] {'docs'}, dimensions={0} | all-to-all | bytes 262144 | tf_op jit(solution)/shard_map/all_to_all | solution.py:404
  22.6 0.0 copy-start
  22.6 0.7 slice.8
  23.3 1.2 slice_reduce_fusion.used_ref
  24.4 28.3 %shard_map.78 = (bf16[8192,256]{1,0:T(8,128)(2,1)}, bf16[8192,256]{1,0:T(8,128)(2,1)}, f32[32,256]{1,0:T(8,128)}) custom-call(s32[8192]{0:T(1024)} %bitcast.5, s32[32]{0:T(128)} %slice_reduce_fusion.used_ref, bf16[8192,256]{1,0:T(8,128)(2,1)} %beta_ref.1), custom_call_target="tpu_custom_call" | custom-call | tf_op jit(solution)/shard_map/pallas_call | solution.py:406
  52.7 0.0 copy-done
  52.7 102.6 %shard_map.79 = (f32[16,256]{1,0:T(8,128)}, f32[512,256]{1,0:T(8,128)}, f32[32,256]{1,0:T(8,128)}) custom-call(s32[32,8,128]{2,1,0:T(8,128)} %copy-done, f32[16,256]{1,0:T(8,128)} %gamma_ref.1, f32[1,256]{1,0:T(1,128)} %bitcast.8, f32[32,256]{1,0:T(8,128)} %get-tuple-element.8.shift_ref, bf16[8192,256]{1,0:T(8,128)(2,1)} %get-tuple-element.9.high_hbm.high_ref, ...), custom_call_target="tpu_custom_call" | custom-call | tf_op jit(solution)/shard_map/pallas_call | solution.py:414
  155.3 0.0 copy-start.1
  155.3 31.7 %shard_map.80 = f32[8192,256]{1,0:T(8,128)} custom-call(s32[8192]{0:T(1024)} %bitcast.6, s32[32]{0:T(128)} %slice_reduce_fusion.used_ref, s32[32,8,128]{2,1,0:T(8,128)} %copy-done, f32[512,256]{1,0:T(8,128)} %get-tuple-element.12.theta_ref, f32[32,256]{1,0:T(8,128)} %get-tuple-element.13.weight_ref, bf16[8192,256]{1,0:T(8,128)(2,1)} %get-tuple-element.9.high_hbm.high_ref, ...), custom_call_target="tpu_custom_call" | custom-call | tf_op jit(solution)/shard_map/pallas_call | solution.py:438
  187.0 0.0 copy-done.1
  187.0 0.6 copy.12
Async XLA Ops:
  22.6 30.1 %copy-start = (s32[32,8,128]{2,1,0:T(8,128)}, s32[32,8,128]{2,1,0:T(8,128)S(1)}, u32[]{:S(2)}) copy-start(s32[32,8,128]{2,1,0:T(8,128)S(1)} %all_to_all.5.req_ref) | copy-start | bytes 393220
  155.3 31.7 %copy-start.1 = (f32[16,256]{1,0:T(8,128)S(1)}, f32[16,256]{1,0:T(8,128)}, u32[]{:S(2)}) copy-start(f32[16,256]{1,0:T(8,128)} %get-tuple-element.16) | copy-start | bytes 49156

commit v3 on v2

v3 whole, which is shorter than its diff:
```python
import functools

import jax
import jax.numpy as jnp
from jax import lax
from jax.experimental import pallas as pl
from jax.experimental.pallas import tpu as pltpu
from jax.sharding import PartitionSpec as P

ITERS = 3
LIFT = 30.0
BF, F32, I32 = jnp.bfloat16, jnp.float32, jnp.int32
NN = (((1,), (0,)), ((), ()))
NT = (((1,), (1,)), ((), ()))
TN = (((0,), (0,)), ((), ()))
MESH = pl.DeviceIdType.MESH
CAP = 256


def dot(a, b, dims=NN):
    return lax.dot_general(a, b, dims, preferred_element_type=F32)


def halves(x):
    high = x.astype(BF)
    return high, (x - high.astype(F32)).astype(BF)


def iota(shape, dim):
    return lax.broadcasted_iota(I32, shape, dim)


def grid_of(owners):
    return {32: 8}.get(owners, owners // 2)


def pack(words, block_ref, row_ref, count_ref, out_ref):
    docs, length = block_ref.shape
    owners = out_ref.shape[0]
    earlier = (iota((length, length), 0) < iota((length, length), 1)).astype(BF)

    def step(d, carry):
        total, offset = carry
        owner, row, count = (ref[pl.ds(d, 1), :] for ref in (block_ref, row_ref, count_ref))
        owner = jnp.where(count > 0, owner, -1)
        member = (iota((owners, length), 0) == owner).astype(F32)
        before = dot(member.astype(BF), earlier) + offset
        rank = jnp.sum(member * before, axis=0, keepdims=True).astype(I32)
        place = (iota((CAP, length), 0) == rank).astype(BF)
        values = jnp.concatenate(
            [
                member * (row % 128).astype(F32),
                member * (row // 128).astype(F32),
                member * (count * docs + d).astype(F32),
            ],
            axis=0,
        ).astype(BF)
        total = total + dot(values, place, NT)
        return total, offset + jnp.sum(member, axis=1, keepdims=True)

    total, offset = lax.fori_loop(
        0, docs, step, (jnp.zeros((3 * owners, CAP), F32), jnp.zeros((owners, 1), F32))
    )
    row = (total[owners : 2 * owners] * 128 + total[:owners]).astype(I32)
    row = jnp.minimum(jnp.maximum(row, 0), words - 1)
    rest = total[2 * owners :].astype(I32)
    used = jnp.broadcast_to(offset, (owners, 128)).astype(I32)
    for half in range(2):
        lanes = slice(half * 128, half * 128 + 128)
        out_ref[:, half, :] = row[:, lanes]
        out_ref[:, 2 + half, :] = rest[:, lanes] % docs
        out_ref[:, 4 + half, :] = rest[:, lanes] // docs
        out_ref[:, 6 + half, :] = used


def exp_digamma(g):
    z = g + 6.0
    total = 1.0 / g
    for i in range(1, 6):
        total = total + 1.0 / (g + float(i))
    inverse = 1.0 / z
    square = inverse * inverse
    series = square * (1 / 12 - square * (1 / 120 - square * (1 / 252 - square * (1 / 240))))
    return jnp.exp(jnp.log(z) - 0.5 * inverse - series - total)


def main_kernel(
    nx, nz, groups,
    block_ref, row_ref, count_ref, gamma_ref, prior_ref, beta_hbm,
    gamma_out, theta_out, weight_out, req, high_hbm, low_hbm,
    request, rows, beta, wide, raw, high_ref, low_ref, theta, own_theta,
    shifts, scales, masses, counts, holders, weights, parts, xparts, zbase, zparts,
    local_sem, rq_send, rq_recv, shift_send, shift_recv, mass_send, mass_recv,
    tz_send, tz_recv, tx_send, tx_recv, sx_send, sx_recv, sz_send, sz_recv,
):
    owners = nx * nz
    docs = gamma_ref.shape[0]
    me, top = lax.axis_index("docs"), lax.axis_index("topics")
    x, z = me // nz, me % nz
    chunks = nz // 2
    size = 2 * nx

    def at_x(d):
        return (x + d) % nx

    def at_z(d):
        return (z + d) % nz

    def block(i):
        return pl.ds(pl.multiple_of(i * docs, docs), docs)

    def slots(s):
        return pl.ds(pl.multiple_of(s * CAP, CAP), CAP)

    def lines(c):
        return pl.ds(pl.multiple_of(c * size, size), size)

    def remote(src, dst, send, recv, **device):
        return pltpu.make_async_remote_copy(
            src_ref=src, dst_ref=dst, send_sem=send, recv_sem=recv, device_id=device, device_id_type=MESH
        )

    def each(n, body, first=1):
        lax.fori_loop(first, n, lambda i, _: (body(i), 0)[1], 0)

    barrier = pltpu.get_barrier_semaphore()
    each(
        owners,
        lambda d: pl.semaphore_signal(
            barrier, inc=1, device_id={"docs": (me + d) % owners}, device_id_type=MESH
        ),
    )
    for d in range(1, groups):
        pl.semaphore_signal(barrier, inc=1, device_id={"topics": (top + d) % groups}, device_id_type=MESH)
    load = pltpu.make_async_copy(beta_hbm, beta, local_sem.at[0])
    load.start()
    pack(beta.shape[0], block_ref, row_ref, count_ref, request)
    first = exp_digamma(gamma_ref[...])
    own_theta[...] = first
    theta[block(me), :] = first
    req[me] = request[me]
    pl.semaphore_wait(barrier, owners - 1 + groups - 1)

    def turn(k):
        return jnp.where(k % 2 == 1, (k + 1) // 2, (nz - k // 2) % nz)

    def rq_copy(d):
        to = (me + d) % owners
        return remote(request.at[to], req.at[me], rq_send.at[d], rq_recv.at[d], docs=to)

    def tz_copy(d):
        return remote(theta.at[block(me)], theta.at[block(me)], tz_send.at[d], tz_recv.at[d], docs=x * nz + at_z(d))

    def tx_copy(dx, dz):
        b = block(x * nz + at_z(nz - dz))
        return remote(theta.at[b], theta.at[b], tx_send.at[dx, dz], tx_recv.at[dx, dz], docs=at_x(dx) * nz + z)

    def sx_copy(dx, dz):
        b = block(at_x(dx) * nz + at_z(dz))
        return remote(parts.at[b], xparts.at[dx, dz], sx_send.at[dx, dz], sx_recv.at[dx, dz], docs=at_x(dx) * nz + z)

    def sz_copy(d):
        return remote(zbase.at[d], zparts.at[d], sz_send.at[d], sz_recv.at[d], docs=x * nz + at_z(d))

    def shift_copy(d, c):
        a = shifts.at[top, lines(c)]
        return remote(a, a, shift_send.at[d, c], shift_recv.at[d, c], topics=(top + d) % groups)

    def mass_copy(p, d, c):
        a = masses.at[p, top, lines(c)]
        return remote(a, a, mass_send.at[d, c], mass_recv.at[p, d, c], topics=(top + d) % groups)

    def source(k, d):
        return at_x(nx - d) * nz + at_z(nz - turn(k))

    def send_theta():
        each(nz, lambda d: tz_copy(d).start())
        for d in range(1, nx):
            tx_copy(d, 0).start()

    def forward(k):
        dz = turn(k)
        tz_copy(dz).wait_recv()
        for d in range(1, nx):
            tx_copy(d, dz).start()

    def mass_of(p, k, d):
        s, q = source(k, d), k * nx + d
        high, low = halves(theta[block(s), :])
        both = dot(jnp.concatenate([high, low], axis=0), high_ref[slots(s), :], NT)
        mass = both[:docs] + both[docs:] + dot(high, low_ref[slots(s), :], NT)
        mine = iota((docs, CAP), 0) == holders[pl.ds(q, 1), :]
        masses[p, top, pl.ds(q, 1), :] = jnp.sum(jnp.where(mine, mass, 0.0), axis=0, keepdims=True)

    def masses_of(p, c):
        def two(k):
            for d in range(1, nx):
                tx_copy(d, turn(k)).wait_recv()
            for d in range(nx):
                mass_of(p, k, d)

        each(2 * c + 2, two, 2 * c)
        each(groups, lambda d: mass_copy(p, d, c).start())

    def sent_theta():
        each(nz, lambda d: tz_copy(d).wait_send())

        def sent(k):
            for d in range(1, nx):
                tx_copy(d, k).wait_send()

        each(nz, sent, 0)

    send_theta()
    each(owners, lambda d: rq_copy(d).start())
    load.wait()

    def widen(i):
        wide[slots(i), :] = beta[slots(i), :].astype(F32)

    each(beta.shape[0] // CAP, widen, 0)
    each(nz, forward)
    each(owners, lambda d: rq_copy(d).wait_recv())
    to_scalars = pltpu.make_async_copy(req.at[:, 0:2, :], rows, local_sem.at[0])
    to_scalars.start()

    def arrange(k):
        for d in range(nx):
            s, q = source(k, d), k * nx + d
            holders[pl.ds(q, 1), :] = jnp.concatenate([req[s, 2:3, :], req[s, 3:4, :]], axis=1)
            counts[pl.ds(q, 1), :] = jnp.concatenate([req[s, 4:5, :], req[s, 5:6, :]], axis=1).astype(F32)

    each(nz, arrange, 0)
    to_scalars.wait()
    lead = (iota((8, 128), 1) == 0).astype(BF)

    def fetch(q):
        s = source(q // nx, q % nx)
        for start in range(0, CAP, 16):
            values = [wide[pl.ds(rows[s, n // 128, n % 128], 1), :] for n in range(start, start + 16)]
            for u in range(16):
                raw[start + u : start + u + 1, :] = values[u]
        value = raw[...]
        peak = jnp.max(value, axis=1, keepdims=True)
        high, low = halves(jnp.exp(value - (peak - LIFT)))
        high_ref[slots(s), :] = high
        low_ref[slots(s), :] = low
        peaks = dot(lead, jnp.broadcast_to(peak, (CAP, 128)).astype(BF), NT)
        shifts[top, pl.ds(q, 1), :] = peaks[:1] - LIFT

    def begin(c):
        each(size * (c + 1), fetch, size * c)
        each(groups, lambda d: shift_copy(d, c).start())
        masses_of(0, c)

    each(chunks, begin, 0)
    keeps = [
        pltpu.make_async_copy(high_ref, high_hbm, local_sem.at[0]),
        pltpu.make_async_copy(low_ref, low_hbm, local_sem.at[1]),
    ]
    for copy in keeps:
        copy.start()
    sent_theta()
    each(owners, lambda d: rq_copy(d).wait_send())

    def scale(c):
        each(groups, lambda d: shift_copy(d, c).wait())
        peak = shifts[0, lines(c), :]
        for t in range(1, groups):
            peak = jnp.maximum(peak, shifts[t, lines(c), :])
        for t in range(groups):
            scales[t, lines(c), :] = jnp.exp(shifts[t, lines(c), :] - peak)

    def weigh(p, c):
        each(groups, lambda d: mass_copy(p, d, c).wait())
        norm = scales[0, lines(c), :] * masses[p, 0, lines(c), :]
        for t in range(1, groups):
            norm = norm + scales[t, lines(c), :] * masses[p, t, lines(c), :]
        weights[lines(c), :] = counts[lines(c), :] * scales[top, lines(c), :] / norm

    def part_of(k, d):
        s, q = source(k, d), k * nx + d
        mine = iota((docs, CAP), 0) == holders[pl.ds(q, 1), :]
        high, low = halves(jnp.where(mine, weights[pl.ds(q, 1), :], 0.0))
        both = dot(jnp.concatenate([high, low], axis=0), high_ref[slots(s), :])
        parts[block(s), :] = both[:docs] + both[docs:] + dot(high, low_ref[slots(s), :])

    def back(k):
        return (nz - turn(k)) % nz

    def parts_of(c):
        def two(k):
            for d in range(nx):
                part_of(k, d)
            for d in range(1, nx):
                sx_copy(d, back(k)).start()

        each(2 * c + 2, two, 2 * c)

    def joined(dz):
        total = parts[block(x * nz + at_z(dz)), :]
        for d in range(1, nx):
            sx_copy(d, dz).wait_recv()
            total = total + xparts[d, dz]
        return total

    def onward(k):
        zbase[back(k)] = joined(back(k))
        sz_copy(back(k)).start()

    def renew(p, prepare):
        def share(c):
            prepare(c)
            weigh(p, c)
            parts_of(c)

        each(chunks, share, 0)
        each(nz, onward)
        total = joined(0)
        for d in range(1, nz):
            sz_copy(d).wait_recv()
            total = total + zparts[d]
        gamma = prior_ref[...] + own_theta[...] * total
        gamma_out[...] = gamma
        new = exp_digamma(gamma)
        own_theta[...] = new
        theta[block(me), :] = new
        send_theta()
        each(nz, lambda d: sz_copy(d).wait_send())

        def sent(k):
            for d in range(1, nx):
                sx_copy(d, k).wait_send()

        each(nz, sent, 0)

    def collect(p):
        each(2, forward)
        each(
            chunks,
            lambda c: (each(jnp.minimum(2 * c + 4, nz), forward, 2 * c + 2), masses_of(p, c)),
            0,
        )
        sent_theta()

    renew(0, scale)

    def sweep(i):
        collect(i % 2)
        renew(i % 2, lambda c: None)

    each(ITERS, sweep)
    collect(ITERS % 2)
    each(chunks, lambda c: weigh(ITERS % 2, c), 0)

    def deliver(k):
        for d in range(nx):
            weight_out[pl.ds(source(k, d), 1), :] = weights[pl.ds(k * nx + d, 1), :]

    each(nz, deliver, 0)
    theta_out[...] = theta[...]
    for copy in keeps:
        copy.wait()


def stats_kernel(docs, rows_ref, used_ref, req_ref, theta_ref, weight_ref, high_hbm, low_hbm, out_hbm, terms, high_ref, low_ref, sem, *sums):
    loads = [
        pltpu.make_async_copy(high_hbm, high_ref, sem.at[0]),
        pltpu.make_async_copy(low_hbm, low_ref, sem.at[1]),
    ]
    for copy in loads:
        copy.start()

    def clear(i, _):
        for total in sums:
            total[pl.ds(pl.multiple_of(i * CAP, CAP), CAP), :] = jnp.zeros((CAP, out_hbm.shape[1]), F32)
        return 0

    lax.fori_loop(0, out_hbm.shape[0] // CAP, clear, 0)
    for copy in loads:
        copy.wait()

    def one(s, _):
        holder = jnp.concatenate([req_ref[s, 2:3, :], req_ref[s, 3:4, :]], axis=1)
        weight = jnp.where(iota((docs, CAP), 0) == holder, weight_ref[pl.ds(s, 1), :], 0.0)
        whigh, wlow = halves(weight)
        thigh, tlow = halves(theta_ref[pl.ds(pl.multiple_of(s * docs, docs), docs), :])
        at = pl.ds(pl.multiple_of(s * CAP, CAP), CAP)
        share = dot(
            jnp.concatenate([whigh, whigh, wlow], axis=0), jnp.concatenate([thigh, tlow, thigh], axis=0), TN
        )
        terms[...] = share * (high_ref[at, :].astype(F32) + low_ref[at, :].astype(F32))

        def eight(j, _):
            base = s * CAP + j * 8
            now = terms.at[pl.ds(pl.multiple_of(j * 8, 8), 8), :]
            rows = [rows_ref[base + u] for u in range(8)]
            for start in range(0, 8, len(sums)):
                news = []
                for k, total in enumerate(sums):
                    u = start + k
                    news.append(total[pl.ds(rows[u], 1), :] + now[u : u + 1, :])
                for k, total in enumerate(sums):
                    total[pl.ds(rows[start + k], 1), :] = news[k]
            return 0

        lax.fori_loop(0, (used_ref[s] + 7) >> 3, eight, 0)
        return 0

    lax.fori_loop(0, used_ref.shape[0], one, 0)

    def finish(i, _):
        at = pl.ds(pl.multiple_of(i * CAP, CAP), CAP)
        sums[0][at, :] = functools.reduce(jnp.add, [total[at, :] for total in sums])
        pltpu.make_async_copy(sums[0].at[at], out_hbm.at[at], sem.at[2]).start()
        return 0

    lax.fori_loop(0, out_hbm.shape[0] // CAP, finish, 0)
    pltpu.make_async_copy(sums[0], out_hbm, sem.at[2]).wait()


VM = pl.BlockSpec(memory_space=pltpu.VMEM)
SM = pl.BlockSpec(memory_space=pltpu.SMEM)
AN = pl.BlockSpec(memory_space=pl.ANY)


def call(kernel, outs, in_specs, out_specs, scratch, **params):
    return pl.pallas_call(
        kernel,
        out_shape=outs,
        in_specs=in_specs,
        out_specs=out_specs,
        scratch_shapes=list(scratch),
        compiler_params=pltpu.CompilerParams(vmem_limit_bytes=60 * 2**20, **params),
    )


def shape(s, t=F32):
    return jax.ShapeDtypeStruct(s, t)


def per_device(log_beta, gamma_init, topic_prior, word_block, word_row, counts):
    docs, length = counts.shape
    words, cols = log_beta.shape
    owners, groups = lax.axis_size("docs"), lax.axis_size("topics")
    nz = grid_of(owners)
    nx = owners // nz
    slots = owners * CAP
    D, V = pltpu.SemaphoreType.DMA, pltpu.VMEM
    block = (docs, cols)
    gamma, theta, weight, req, high, low = call(
        functools.partial(main_kernel, nx, nz, groups),
        [
            shape(block), shape((owners * docs, cols)), shape((owners, CAP)), shape((owners, 8, 128), I32),
            shape((slots, cols), BF), shape((slots, cols), BF),
        ],
        [VM] * 5 + [AN],
        [VM] * 4 + [AN] * 2,
        [
            V((owners, 8, 128), I32),
            pltpu.SMEM((owners, 2, 128), I32),
            V((words, cols), BF),
            V((words, cols), F32),
            V((CAP, cols), F32),
            V((slots, cols), BF),
            V((slots, cols), BF),
            V((owners * docs, cols), F32),
            V(block, F32),
            V((groups, owners, CAP), F32),
            V((groups, owners, CAP), F32),
            V((2, groups, owners, CAP), F32),
            V((owners, CAP), F32),
            V((owners, CAP), I32),
            V((owners, CAP), F32),
            V((owners * docs, cols), F32),
            V((nx, nz, *block), F32),
            V((nz, *block), F32),
            V((nz, *block), F32),
            D((2,)), D((owners,)), D((owners,)), D((groups, nz // 2)), D((groups, nz // 2)),
            D((groups, nz // 2)), D((2, groups, nz // 2)),
            D((nz,)), D((nz,)), D((nx, nz)), D((nx, nz)), D((nx, nz)), D((nx, nz)), D((nz,)), D((nz,)),
        ],
        collective_id=1,
        has_side_effects=True,
    )(word_block[:, :, 0], word_row, counts, gamma_init, topic_prior[None, :], log_beta)
    rows, used = req[:, :2, :].reshape(slots), req[:, 6, 0]
    stats = call(
        functools.partial(stats_kernel, docs),
        shape((words, cols)),
        [SM, SM] + [VM] * 3 + [AN] * 2,
        AN,
        [V((CAP, cols), F32), V((slots, cols), BF), V((slots, cols), BF), D((3,))]
        + [V((words, cols), F32)] * 4,
    )(rows, used, req, theta, weight, high, low)
    return gamma, stats


def solution(mesh):
    return jax.shard_map(
        per_device,
        mesh=mesh,
        in_specs=(
            P("docs", "topics"),
            P("docs", "topics"),
            P("topics"),
            P("docs", None, None),
            P("docs", None),
            P("docs", None),
        ),
        out_specs=(P("docs", "topics"), P("docs", "topics")),
        check_vma=False,
    )
```

time: 190 us -> 174 us (0.916)
  the two profiles are of different devices: /device:TPU:167 before, /device:TPU:2 now
where the time goes in v3:
time: 174 us; the launch traced here: 172 us
  Pallas kernels  165 us (95%)
  local copies, waits for them, and re-layouts  5.53 us (3%)
    pallas_call x1, Pallas kernels, per_device(): call(functools.partial(main_kernel, nx, nz, groups), [shape(block), shape...  137 us
    pallas_call x1, Pallas kernels, per_device(): call(functools.partial(stats_kernel, docs), shape((words, cols)), [SM, SM...  27.9 us
    slice x2, local copies, waits for them, and re-layouts, per_device(): rows, used = (req[:, :2, :].reshape(slots), req[:, 6, 0])  3.6 us

profile of v3, /device:TPU:2, one launch (start us, length us, event | category | flops | bytes accessed | tf_op | source)
XLA Modules:
  0.0 171.6 jit_solution(5589895093760489215)
XLA Ops:
  0.6 1.3 copy.10
  2.0 137.5 %shard_map.77 = (f32[16,256]{1,0:T(8,128)}, f32[512,256]{1,0:T(8,128)}, f32[32,256]{1,0:T(8,128)}, s32[32,8,128]{2,1,0:T(8,128)}, bf16[8192,256]{1,0:T(8,128)(2,1)}, /*index=5*/bf16[8192,256]{1,0:T(8,128)(2,1)}) custom-call(s32[16,256]{1,0:T(8,128)} %bitcast.6, s32[16,256]{1,0:T(8,128)} %row_ref.1, s32[16,256]{1,0:T(8,128)} %count_ref.1, ...), custom_call_target="tpu_custom_call" | custom-call | tf_op jit(solution)/shard_map/pallas_call | solution.py:451
  139.5 2.1 %slice_reduce_fusion.used_ref = s32[32]{0:T(128)} fusion(s32[32,8,128]{2,1,0:T(8,128)} %get-tuple-element.9.req_ref), kind=kLoop, calls=%fused_computation.1 | loop fusion | bytes 256 | tf_op jit(solution)/shard_map/slice | solution.py:486
  141.5 1.5 slice.6
  143.0 0.0 copy-start
  143.1 27.9 %shard_map.78 = f32[8192,256]{1,0:T(8,128)} custom-call(s32[8192]{0:T(1024)} %bitcast.5, s32[32]{0:T(128)} %slice_reduce_fusion.used_ref, s32[32,8,128]{2,1,0:T(8,128)} %get-tuple-element.9.req_ref, f32[512,256]{1,0:T(8,128)} %get-tuple-element.10.theta_ref, f32[32,256]{1,0:T(8,128)} %get-tuple-element.11.weight_ref, ...), custom_call_target="tpu_custom_call" | custom-call | tf_op jit(solution)/shard_map/pallas_call | solution.py:487
  171.0 0.0 copy-done
  171.0 0.6 copy.12
Async XLA Ops:
  143.0 27.9 %copy-start = (f32[16,256]{1,0:T(8,128)S(1)}, f32[16,256]{1,0:T(8,128)}, u32[]{:S(2)}) copy-start(f32[16,256]{1,0:T(8,128)} %get-tuple-element.16) | copy-start | bytes 49156
